TPU v7x, 32 devices: a whole 2x2x4 slice. The times are simulated.
32 devices in a mesh: pole: 2 (over y), prow: 4 (over z), pcol: 4 (over x, core).
Axes of the slice: x: 2, y: 2, z: 4, core: 2. Of those that a mesh axis runs over, the one named last changes fastest.
Arguments:
- ainv_anc: bfloat16 [2, 4096, 2048], P(None, ('pole', 'prow'), 'pcol'), parts along dimension 1, may hold values from -6 to 6
- panel: bfloat16 [2, 8, 1024, 256], P(None, 'pole', ('pcol', 'prow')), parts along dimension 1, may hold values from -6 to 6
- u_inv: bfloat16 [2, 8, 256, 256], P(None, 'pole'), parts along dimension 1, may hold values from -0.01171875 to 0.01171875
- k_inv: float32 [2, 8, 256, 256], P(None, ('pole', 'pcol')), parts along dimension 1, may hold values from -6 to 6
- structure: int32 [4, 4], replicated, may hold values from -1 to 7, as said below
Outputs:
- sel_inv: float32 [2, 4096, 1024], P(None, ('pole', 'prow'), 'pcol'), parts along dimension 1
- diag_inv: float32 [2, 8, 256, 256], P(None, ('pole', 'pcol')), parts along dimension 1
There are 2 independent parts, one for each index of `pole`. A program takes and returns all parts, laid end to end along the dimension named above; an argument that names none is the same for every part. Nothing has to cross between parts.
Inputs may be any that keep to these rules, and one draw needn't show every extreme that they name: `structure`: slots g * 1 to (g + 1) * 1 - 1 of row k hold distinct blocks of g * 2 to (g + 1) * 2 - 1 in rising order, followed by -1 for empty slots; each such group of each row holds at least one block, and for every g some row fills all 1 slots of group g.
All inputs are finite; a program needn't handle non-finite values.
Results may differ from a plain program's by a relative error of at most 0.005.
Values may be sent and summed in bfloat16 or wider, within the bound.
No kernel may reach another device: no remote copies, remote signals or barrier semaphores. Data moves between devices by JAX's collectives and lax.ppermute only.
A program may use at most 128 MiB of HBM per device.

v0:
```python
import jax
import jax.numpy as jnp
from jax import lax
from jax.sharding import PartitionSpec as P


def complex_quad(z_part, s_part):
    highest = lax.Precision.HIGHEST

    def single(left, right):
        return jnp.einsum("kra,rkb->kab", left, right, precision=highest)

    real = single(z_part[0], s_part[0]) - single(z_part[1], s_part[1])
    imag = single(z_part[0], s_part[1]) + single(z_part[1], s_part[0])
    return jnp.stack([real, imag])


def local(ainv_anc, panel, u_inv, k_inv, structure):
    block_width = u_inv.shape[-1]
    total_k = u_inv.shape[1]
    own_k = k_inv.shape[1]
    n_cols = lax.axis_size("pcol")
    row_here = lax.axis_index("prow")
    col_here = lax.axis_index("pcol")
    row_blocks = ainv_anc.shape[1] // block_width
    group_blocks = ainv_anc.shape[2] // block_width
    group_slots = structure.shape[1] // n_cols
    rows_all = row_blocks * block_width
    col_struct = lax.dynamic_slice_in_dim(structure, col_here * group_slots, group_slots, 1)
    slot_live = col_struct >= 0
    slot_pos = col_struct - col_here * group_blocks
    first_block = row_here * row_blocks
    target = first_block + jnp.arange(row_blocks, dtype=jnp.int32)
    rows_in = lax.all_gather(panel, "prow", axis=2, tiled=True)

    def single(left, right):
        return jnp.einsum("knb,kbc->knc", left, right, preferred_element_type=jnp.float32)

    real = single(rows_in[0], u_inv[0]) - single(rows_in[1], u_inv[1])
    imag = single(rows_in[0], u_inv[1]) + single(rows_in[1], u_inv[0])
    placed = jnp.stack([real, imag]).astype(jnp.bfloat16)
    placed = placed.reshape(2, total_k, group_slots, block_width, block_width)
    placed = jnp.where(slot_live[None, :, :, None, None], placed, jnp.zeros((), jnp.bfloat16))
    block_ids = jnp.arange(group_blocks, dtype=jnp.int32)
    pick_table = (slot_pos[:, :, None] == block_ids[None, None, :]).astype(jnp.bfloat16)
    ainv_blocks = ainv_anc.reshape(2, rows_all, group_blocks, block_width)

    def one_node(items):
        table_k, rows_k = items
        picked = jnp.einsum(
            "sg,cigw->cisw", table_k, ainv_blocks, preferred_element_type=jnp.float32
        )
        picked = picked.astype(jnp.bfloat16).reshape(2, rows_all, group_slots * block_width)
        right = rows_k.reshape(2, group_slots * block_width, block_width)
        real = jnp.dot(picked[0], right[0], preferred_element_type=jnp.float32) - jnp.dot(
            picked[1], right[1], preferred_element_type=jnp.float32
        )
        imag = jnp.dot(picked[0], right[1], preferred_element_type=jnp.float32) + jnp.dot(
            picked[1], right[0], preferred_element_type=jnp.float32
        )
        return jnp.stack([real, imag])

    per_node = lax.map(one_node, (pick_table, jnp.moveaxis(placed, 1, 0)))
    partial_value = jnp.transpose(per_node, (1, 2, 0, 3))
    row_table = (col_struct[:, None, :] == target[None, :, None]).astype(jnp.bfloat16)
    z_rows = jnp.einsum("kts,ckswb->cktwb", row_table, placed, preferred_element_type=jnp.float32)
    z_rows = z_rows.astype(jnp.bfloat16).reshape(2, total_k, rows_all, block_width)
    summed = lax.psum_scatter(
        partial_value.reshape(2, rows_all, total_k * block_width),
        "pcol",
        scatter_dimension=2,
        tiled=True,
    )
    own_struct = lax.dynamic_slice_in_dim(structure, col_here * own_k, own_k, 0)
    member = jnp.any(own_struct[:, :, None] == target[None, None, :], axis=1)
    selected = -summed.reshape(2, row_blocks, block_width, own_k, block_width)
    selected = jnp.where(member.T[None, :, None, :, None], selected, 0.0)
    sel_inv = selected.reshape(2, rows_all, own_k * block_width)
    received = lax.all_to_all(z_rows, "pcol", split_axis=1, concat_axis=1, tiled=True)
    z_own = (
        received.astype(jnp.float32).reshape(2, n_cols, own_k, rows_all, block_width).sum(axis=1)
    )
    quad_term = complex_quad(z_own, selected.reshape(2, rows_all, own_k, block_width))
    total_sum = lax.psum(quad_term, "prow")
    diag_inv = k_inv - total_sum
    return (sel_inv, diag_inv)


def solution(mesh):
    placed = (
        P(None, ("pole", "prow"), "pcol"),
        P(None, "pole", ("pcol", "prow"), None),
        P(None, "pole", None, None),
        P(None, ("pole", "pcol"), None, None),
        P(),
    )
    return jax.shard_map(
        local,
        mesh=mesh,
        in_specs=placed,
        out_specs=(P(None, ("pole", "prow"), "pcol"), P(None, ("pole", "pcol"), None, None)),
        check_vma=False,
    )
```

profile of v0, /device:TPU:0, one launch (start us, length us, event | category | flops | bytes accessed | tf_op | source)
XLA Modules:
  0.0 170.8 jit_solution(10218093751577018464)
XLA Ops:
  8.0 1.3 reshape.276
  11.2 29.1 %all-gather.2.cloned.1.call-done = bf16[2,4,256,256]{3,2,1,0:T(8,128)(2,1)} async-done(((bf16[2,4,64,256]{3,2,1,0:T(8,128)(2,1)}), bf16[2,4,256,256]{3,2,1,0:T(8,128)(2,1)}) %all-gather.2.cloned.1.call-update) | async-done | bytes 1048592 | tf_op jit(solution)/shard_map/all_gather | solution.py:34
  40.3 1.6 fusion.13
  41.9 1.3 fusion.17
  44.1 13.4 %while.10 = (s32[]{:T(128)}, f32[4,2,512,256]{3,2,1,0:T(8,128)}, bf16[4,1,2]{2,1,0:T(2,128)(2,1)S(1)}, bf16[2,512,2,256]{3,2,1,0:T(2,128)(2,1)S(1)}, bf16[4,2,1,256,256]{4,3,0,2,1:T(8,128)(2,1)S(1)}, /*index=5*/s32[]{:T(128)}) while((s32[]{:T(128)}, f32[4,2,512,256]{3,2,1,0:T(8,128)}, bf16[4,1,2]{2,1,0:T(2,128)(2,1)S(1)}, ...), condition=%wide.region_2.3_spmd, body=%wide.region_1.2_spmd.sunk | while | flops 270008320 | bytes 9962073 | solution.py:63
  44.1 1.2 fusion.42
  46.4 1.0 fusion.47
  47.4 1.2 fusion.42
  49.7 1.1 fusion.47
  50.8 1.2 fusion.42
  53.1 1.1 fusion.47
  54.2 1.2 fusion.42
  56.4 1.0 fusion.47
  57.5 4.8 %copy.21 = f32[4,2,64,8,256]{4,3,0,2,1:T(8,128)} copy(f32[4,2,64,8,256]{4,3,2,1,0:T(8,128)} %bitcast.135) | data formatting | bytes 8388608 | tf_op jit(solution)/shard_map/reshape | solution.py:69
  63.0 1.5 copy.17
  64.5 3.8 %all-to-all-start = ((bf16[2,4,512,256]{3,2,0,1:T(8,128)(2,1)}), bf16[2,4,512,256]{3,2,0,1:T(8,128)(2,1)S(1)}, u32[]{:S(2)}, u32[]{:S(2)}) async-start(bf16[2,4,512,256]{3,2,0,1:T(8,128)(2,1)} %copy.17), calls=%async_computation.1 | async-start | bytes 4194304 | tf_op jit(solution)/shard_map/all_to_all | solution.py:79
  69.2 36.9 %all-to-all-done = bf16[2,4,512,256]{3,2,0,1:T(8,128)(2,1)S(1)} async-done(((bf16[2,4,512,256]{3,2,0,1:T(8,128)(2,1)}), bf16[2,4,512,256]{3,2,0,1:T(8,128)(2,1)S(1)}, u32[]{:S(2)}, u32[]{:S(2)}) %all-to-all-start) | async-done | bytes 2097184 | tf_op jit(solution)/shard_map/all_to_all | solution.py:79
  106.4 11.5 %reduce-scatter.2.cloned.1.call-done = f32[2,512,256]{2,1,0:T(8,128)} async-done(((f32[2,512,1024]{2,1,0:T(8,128)}), f32[2,512,256]{2,1,0:T(8,128)}) %reduce-scatter.2.cloned.1.call-update) | async-done | bytes 1048592 | tf_op jit(solution)/shard_map/reduce_scatter | solution.py:68
  117.9 2.3 %fusion.26 = (f32[2,512,256]{2,1,0:T(8,128)S(1)}, f32[2,512,256]{2,1,0:T(8,128)}) fusion(f32[2,512,256]{2,1,0:T(8,128)} %reduce-scatter.2.cloned.1.call-done, pred[512]{0:T(512)(128)(4,1)S(1)} %broadcast_in_dim.53), kind=kLoop, calls=%fused_computation.59 | loop fusion | flops 524288 | bytes 3146240 | tf_op jit(solution)/shard_map/neg | solution.py:76
  120.5 1.0 fusion.19
  122.5 1.0 fusion.10
  123.5 1.0 fusion.11
  125.4 37.0 %all-reduce.2.cloned.1.call-done = f32[2,1,256,256]{3,2,1,0:T(8,128)} async-done(((f32[2,1,256,256]{3,2,1,0:T(8,128)}), f32[2,1,256,256]{3,2,1,0:T(8,128)}) %all-reduce.2.cloned.1.call-update) | async-done | bytes 524304 | tf_op jit(solution)/shard_map/psum | solution.py:84
  162.4 1.9 %sub.26 = f32[2,1,256,256]{3,2,1,0:T(8,128)} subtract(f32[2,1,256,256]{3,2,1,0:T(8,128)S(1)} %copy-done.2, f32[2,1,256,256]{3,2,1,0:T(8,128)} %all-reduce.2.cloned.1.call-done) | non-fusion elementwise | flops 131072 | bytes 1572864 | tf_op jit(solution)/shard_map/sub | solution.py:85
  (56 shorter events, 11.5 us)
Async XLA Ops:
  7.2 34.7 %copy-start = (bf16[2,4,256,256]{3,2,1,0:T(8,128)(2,1)S(1)}, bf16[2,4,256,256]{3,2,1,0:T(8,128)(2,1)}, u32[]{:S(2)}) copy-start(bf16[2,4,256,256]{3,2,1,0:T(8,128)(2,1)} %param.9) | copy-start | bytes 3145732
  7.2 33.1 %all-gather.2.cloned.1.call-start = ((), (), s32[]{:S(2)}) async-start(), calls=%async_computation.2 | async-start | bytes 1310720 | tf_op jit(solution)/shard_map/all_gather | solution.py:34
  7.9 110.0 %reduce-scatter.2.cloned.1.call-start = ((), (), s32[]{:S(2)}) async-start(), calls=%async_computation.3 | async-start | bytes 5242880 | tf_op jit(solution)/shard_map/reduce_scatter | solution.py:68
  40.3 3.0 %copy-start.1 = (bf16[2,4,256,256]{3,2,1,0:T(8,128)(2,1)S(1)}, bf16[2,4,256,256]{3,2,1,0:T(8,128)(2,1)}, u32[]{:S(2)}) copy-start(bf16[2,4,256,256]{3,2,1,0:T(8,128)(2,1)} %all-gather.2.cloned.1.call-done) | copy-start | bytes 3145732
  64.5 41.6 %all-to-all-start = ((bf16[2,4,512,256]{3,2,0,1:T(8,128)(2,1)}), bf16[2,4,512,256]{3,2,0,1:T(8,128)(2,1)S(1)}, u32[]{:S(2)}, u32[]{:S(2)}) async-start(bf16[2,4,512,256]{3,2,0,1:T(8,128)(2,1)} %copy.17), calls=%async_computation.1 | async-start | bytes 4194304 | tf_op jit(solution)/shard_map/all_to_all | solution.py:79
  68.2 94.1 %all-reduce.2.cloned.1.call-start = ((), (), s32[]{:S(2)}) async-start(), calls=%async_computation.4 | async-start | bytes 1048576 | tf_op jit(solution)/shard_map/psum | solution.py:84
  120.4 41.9 %copy-start.2 = (f32[2,1,256,256]{3,2,1,0:T(8,128)S(1)}, f32[2,1,256,256]{3,2,1,0:T(8,128)}, u32[]{:S(2)}) copy-start(f32[2,1,256,256]{3,2,1,0:T(8,128)} %param.10) | copy-start | bytes 1572868
Sparse Core Ops, SparseCore 0:
  9.6 30.6 all-gather.1
  62.4 55.4 reduce-scatter.1
  125.5 36.8 all-reduce.1
where the time goes:
time: 171 us
  waiting for transfers between devices  115 us (67%)
  matrix products  16.1 us (9%)
  between operations  13.9 us (8%)
  other arithmetic  12.6 us (7%)
  local copies, waits for them, and re-layouts  8.88 us (5%)
  starting transfers between devices  3.88 us (2%)
    psum x1, waiting for transfers between devices, local(): total_sum = lax.psum(quad_term, 'prow')  37 us
    all_to_all x1, waiting for transfers between devices, local(): lax.all_to_all(z_rows, 'pcol', split_axis=1, concat_axis=1, tiled=True)  36.9 us
    all_gather x1, waiting for transfers between devices, local(): rows_in = lax.all_gather(panel, 'prow', axis=2, tiled=True)  29.1 us
    reduce_scatter x1, waiting for transfers between devices, local(): lax.psum_scatter(partial_value.reshape(2, rows_all, total_k * block_width...  11.5 us
    dot_general x4, matrix products, one_node(): jnp.einsum('sg,cigw->cisw', table_k, ainv_blocks, preferred_element_type=...  4.94 us
    reshape x1, local copies, waits for them, and re-layouts, local(): partial_value.reshape(2, rows_all, total_k * block_width)  4.76 us
    dynamic_update_slice x4, other arithmetic, local(): per_node = lax.map(one_node, (pick_table, jnp.moveaxis(placed, 1, 0)))  4.27 us
    dot_general x4, matrix products, single(): return jnp.einsum('kra,rkb->kab', left, right, precision=highest)  4.02 us
  transfers between devices with their start and end apart: 4, of which 4 were waited for; matrix products, arithmetic and copies ran while one was open for 4% of the time, Pallas kernels for 0%

commit v1 on v0

--- a/solution.py
+++ b/solution.py
@@ -81,7 +81,11 @@
         received.astype(jnp.float32).reshape(2, n_cols, own_k, rows_all, block_width).sum(axis=1)
     )
     quad_term = complex_quad(z_own, selected.reshape(2, rows_all, own_k, block_width))
-    total_sum = lax.psum(quad_term, "prow")
+    total_sum = quad_term
+    for hop in (1, 2):
+        total_sum = total_sum + lax.ppermute(
+            total_sum, "prow", [(dev, dev ^ hop) for dev in range(4)]
+        )
     diag_inv = k_inv - total_sum
     return (sel_inv, diag_inv)
 

time: 171 us -> 172 us (level)
  starting transfers between devices: 3.88 us -> 6.97 us
    psum x1 -> x0, waiting for transfers between devices: 37 us -> none  [local(): total_sum = lax.psum(quad_term, 'prow')]
    ppermute x0 -> x2, waiting for transfers between devices: none -> 35.9 us  [local(): lax.ppermute(total_sum, 'prow', [(dev, dev ^ hop) for dev in range(4)])]
    ppermute x0 -> x2, starting transfers between devices: none -> 3.13 us  [local(): lax.ppermute(total_sum, 'prow', [(dev, dev ^ hop) for dev in range(4)])]
  transfers between devices with their start and end apart: 4 -> 5, of which waited for: 4 -> 5; matrix products, arithmetic and copies ran while one was open for 4% -> 4% of each run, Pallas kernels for 0% -> 0%
where the time goes in v1:
time: 172 us; the launch traced here: 171 us
  waiting for transfers between devices  114 us (66%)
  matrix products  16.1 us (9%)
  between operations  14.2 us (8%)
  other arithmetic  10.9 us (6%)
  local copies, waits for them, and re-layouts  8.88 us (5%)
  starting transfers between devices  6.97 us (4%)
    all_to_all x1, waiting for transfers between devices, local(): lax.all_to_all(z_rows, 'pcol', split_axis=1, concat_axis=1, tiled=True)  37 us
    ppermute x2, waiting for transfers between devices, local(): lax.ppermute(total_sum, 'prow', [(dev, dev ^ hop) for dev in range(4)])  35.9 us
    all_gather x1, waiting for transfers between devices, local(): rows_in = lax.all_gather(panel, 'prow', axis=2, tiled=True)  29.1 us
    reduce_scatter x1, waiting for transfers between devices, local(): lax.psum_scatter(partial_value.reshape(2, rows_all, total_k * block_width...  11.5 us
    dot_general x4, matrix products, one_node(): jnp.einsum('sg,cigw->cisw', table_k, ainv_blocks, preferred_element_type=...  4.94 us
    reshape x1, local copies, waits for them, and re-layouts, local(): partial_value.reshape(2, rows_all, total_k * block_width)  4.76 us
    dynamic_update_slice x4, other arithmetic, local(): per_node = lax.map(one_node, (pick_table, jnp.moveaxis(placed, 1, 0)))  4.27 us
    dot_general x4, matrix products, single(): return jnp.einsum('kra,rkb->kab', left, right, precision=highest)  4.02 us
  transfers between devices with their start and end apart: 5, of which 5 were waited for; matrix products, arithmetic and copies ran while one was open for 4% of the time, Pallas kernels for 0%

profile of v1, /device:TPU:0, one launch (start us, length us, event | category | flops | bytes accessed | tf_op | source)
XLA Modules:
  0.0 171.4 jit_solution(17750377855515778440)
XLA Ops:
  8.0 1.3 reshape.276
  11.2 29.1 %all-gather.2.cloned.1.call-done = bf16[2,4,256,256]{3,2,1,0:T(8,128)(2,1)} async-done(((bf16[2,4,64,256]{3,2,1,0:T(8,128)(2,1)}), bf16[2,4,256,256]{3,2,1,0:T(8,128)(2,1)}) %all-gather.2.cloned.1.call-update) | async-done | bytes 1048592 | tf_op jit(solution)/shard_map/all_gather | solution.py:34
  40.3 1.6 fusion.13
  41.9 1.3 fusion.17
  44.1 13.4 %while.10 = (s32[]{:T(128)}, f32[4,2,512,256]{3,2,1,0:T(8,128)}, bf16[4,1,2]{2,1,0:T(2,128)(2,1)S(1)}, bf16[2,512,2,256]{3,2,1,0:T(2,128)(2,1)S(1)}, bf16[4,2,1,256,256]{4,3,0,2,1:T(8,128)(2,1)S(1)}, /*index=5*/s32[]{:T(128)}) while((s32[]{:T(128)}, f32[4,2,512,256]{3,2,1,0:T(8,128)}, bf16[4,1,2]{2,1,0:T(2,128)(2,1)S(1)}, ...), condition=%wide.region_2.3_spmd, body=%wide.region_1.2_spmd.sunk | while | flops 270008320 | bytes 9962073 | solution.py:63
  44.1 1.2 fusion.43
  46.4 1.0 fusion.48
  47.4 1.2 fusion.43
  49.7 1.1 fusion.48
  50.8 1.2 fusion.43
  53.1 1.1 fusion.48
  54.2 1.2 fusion.43
  56.4 1.0 fusion.48
  57.5 4.8 %copy.21 = f32[4,2,64,8,256]{4,3,0,2,1:T(8,128)} copy(f32[4,2,64,8,256]{4,3,2,1,0:T(8,128)} %bitcast.135) | data formatting | bytes 8388608 | tf_op jit(solution)/shard_map/reshape | solution.py:69
  63.0 1.5 copy.17
  64.5 3.8 %all-to-all-start = ((bf16[2,4,512,256]{3,2,0,1:T(8,128)(2,1)}), bf16[2,4,512,256]{3,2,0,1:T(8,128)(2,1)S(1)}, u32[]{:S(2)}, u32[]{:S(2)}) async-start(bf16[2,4,512,256]{3,2,0,1:T(8,128)(2,1)} %copy.17), calls=%async_computation.1 | async-start | bytes 4194304 | tf_op jit(solution)/shard_map/all_to_all | solution.py:79
  69.1 37.0 %all-to-all-done = bf16[2,4,512,256]{3,2,0,1:T(8,128)(2,1)S(1)} async-done(((bf16[2,4,512,256]{3,2,0,1:T(8,128)(2,1)}), bf16[2,4,512,256]{3,2,0,1:T(8,128)(2,1)S(1)}, u32[]{:S(2)}, u32[]{:S(2)}) %all-to-all-start) | async-done | bytes 2097184 | tf_op jit(solution)/shard_map/all_to_all | solution.py:79
  106.4 11.5 %reduce-scatter.2.cloned.1.call-done = f32[2,512,256]{2,1,0:T(8,128)} async-done(((f32[2,512,1024]{2,1,0:T(8,128)}), f32[2,512,256]{2,1,0:T(8,128)}) %reduce-scatter.2.cloned.1.call-update) | async-done | bytes 1048592 | tf_op jit(solution)/shard_map/reduce_scatter | solution.py:68
  117.9 2.3 %fusion.27 = (f32[2,512,256]{2,1,0:T(8,128)S(1)}, f32[2,512,256]{2,1,0:T(8,128)}) fusion(f32[2,512,256]{2,1,0:T(8,128)} %reduce-scatter.2.cloned.1.call-done, pred[512]{0:T(512)(128)(4,1)S(1)} %broadcast_in_dim.53), kind=kLoop, calls=%fused_computation.61 | loop fusion | flops 524288 | bytes 3146240 | tf_op jit(solution)/shard_map/neg | solution.py:76
  123.5 1.0 fusion.11
  124.6 1.4 collective-permute-start
  126.0 12.5 %collective-permute-done = f32[2,1,256,256]{3,2,1,0:T(8,128)S(1)} collective-permute-done((f32[2,1,256,256]{3,2,1,0:T(8,128)S(1)}, f32[2,1,256,256]{3,2,1,0:T(8,128)S(1)}, u32[]{:S(2)}, u32[]{:S(2)}) %collective-permute-start) | collective-permute-done | bytes 524320 | tf_op jit(solution)/shard_map/ppermute | solution.py:86
  138.5 1.7 collective-permute-start.1
  140.2 23.4 %collective-permute-done.1 = f32[2,1,256,256]{3,2,1,0:T(8,128)S(1)} collective-permute-done((f32[2,1,256,256]{3,2,1,0:T(8,128)S(1)}, f32[2,1,256,256]{3,2,1,0:T(8,128)S(1)}, u32[]{:S(2)}, u32[]{:S(2)}) %collective-permute-start.1) | collective-permute-done | bytes 524320 | tf_op jit(solution)/shard_map/ppermute | solution.py:86
  (58 shorter events, 13.6 us)
Async XLA Ops:
  7.2 34.7 %copy-start = (bf16[2,4,256,256]{3,2,1,0:T(8,128)(2,1)S(1)}, bf16[2,4,256,256]{3,2,1,0:T(8,128)(2,1)}, u32[]{:S(2)}) copy-start(bf16[2,4,256,256]{3,2,1,0:T(8,128)(2,1)} %param.9) | copy-start | bytes 3145732
  7.2 33.1 %all-gather.2.cloned.1.call-start = ((), (), s32[]{:S(2)}) async-start(), calls=%async_computation.2 | async-start | bytes 1310720 | tf_op jit(solution)/shard_map/all_gather | solution.py:34
  7.9 110.0 %reduce-scatter.2.cloned.1.call-start = ((), (), s32[]{:S(2)}) async-start(), calls=%async_computation.3 | async-start | bytes 5242880 | tf_op jit(solution)/shard_map/reduce_scatter | solution.py:68
  40.3 3.0 %copy-start.1 = (bf16[2,4,256,256]{3,2,1,0:T(8,128)(2,1)S(1)}, bf16[2,4,256,256]{3,2,1,0:T(8,128)(2,1)}, u32[]{:S(2)}) copy-start(bf16[2,4,256,256]{3,2,1,0:T(8,128)(2,1)} %all-gather.2.cloned.1.call-done) | copy-start | bytes 3145732
  64.5 41.6 %all-to-all-start = ((bf16[2,4,512,256]{3,2,0,1:T(8,128)(2,1)}), bf16[2,4,512,256]{3,2,0,1:T(8,128)(2,1)S(1)}, u32[]{:S(2)}, u32[]{:S(2)}) async-start(bf16[2,4,512,256]{3,2,0,1:T(8,128)(2,1)} %copy.17), calls=%async_computation.1 | async-start | bytes 4194304 | tf_op jit(solution)/shard_map/all_to_all | solution.py:79
  120.4 43.2 %copy-start.2 = (f32[2,1,256,256]{3,2,1,0:T(8,128)S(1)}, f32[2,1,256,256]{3,2,1,0:T(8,128)}, u32[]{:S(2)}) copy-start(f32[2,1,256,256]{3,2,1,0:T(8,128)} %param.10) | copy-start | bytes 1572868
  124.6 13.9 %collective-permute-start = (f32[2,1,256,256]{3,2,1,0:T(8,128)S(1)}, f32[2,1,256,256]{3,2,1,0:T(8,128)S(1)}, u32[]{:S(2)}, u32[]{:S(2)}) collective-permute-start(f32[2,1,256,256]{3,2,1,0:T(8,128)S(1)} %pad_maximum_fusion), channel_id=1, source_target_pairs={{0,4},{4,0},{8,12},{12,8},{1,5},{5,1},{9,13},{13,9},{2,6},{6,2},{1... | collective-permute-start | bytes 1572872 | tf_op jit(solution)/shard_map/ppermute | solution.py:86
  138.5 25.1 %collective-permute-start.1 = (f32[2,1,256,256]{3,2,1,0:T(8,128)S(1)}, f32[2,1,256,256]{3,2,1,0:T(8,128)S(1)}, u32[]{:S(2)}, u32[]{:S(2)}) collective-permute-start(f32[2,1,256,256]{3,2,1,0:T(8,128)S(1)} %fusion.25), channel_id=1, source_target_pairs={{0,8},{4,12},{8,0},{12,4},{1,9},{5,13},{9,1},{13,5},{2,10},{6,14},... | collective-permute-start | bytes 1572872 | tf_op jit(solution)/shard_map/ppermute | solution.py:86
Sparse Core Ops, SparseCore 0:
  9.6 30.6 all-gather.1
  62.4 55.4 reduce-scatter.1
